TPU v7x, 32 devices: a whole 2x2x4 slice. The times are simulated.
32 devices in a mesh: ulysses: 8 (over z, x), blk: 4 (over y, core).
Axes of the slice: x: 2, y: 2, z: 4, core: 2. Of those that a mesh axis runs over, the one named last changes fastest.
Arguments:
- queries: bfloat16 [4, 512, 4096], P('blk', 'ulysses'), may hold values from -6 to 6
- key_rows: bfloat16 [4, 512, 1024], P('blk', 'ulysses'), may hold values from -6 to 6
- value_rows: bfloat16 [4, 512, 1024], P('blk', 'ulysses'), may hold values from -6 to 6
- tile_segment: int32 [16], replicated, may hold values from 0 to 3, never falling along the last dimension, each value on 1 to 8 neighbouring positions
Outputs:
- attended: bfloat16 [4, 512, 4096], P('blk', 'ulysses')
Inputs may be any that keep to these rules, and one draw needn't show every extreme that they name: `tile_segment`: segment numbers never fall along the sequence and each segment covers 1 to 8 tiles.
All inputs are finite; a program needn't handle non-finite values.
Results may differ from a plain program's by a relative error of at most 0.0045.
Values may be sent and summed in bfloat16 or wider, within the bound.
A program may use at most 64 MiB of HBM per device.

v0:
```python
import math
import jax
import jax.numpy as jnp
from jax import lax
from jax.sharding import PartitionSpec as P

HEAD_DIM = 128
TILE = 128
masked_score = -1e30


def segment_of(positions, tile_segment):
    tiles_total = tile_segment.shape[0]
    matches = (positions // TILE)[:, None] == jnp.arange(tiles_total, dtype=jnp.int32)[None, :]
    return jnp.sum(jnp.where(matches, tile_segment[None, :], 0), axis=1)


def visible(query_pos, query_seg, key_pos, key_seg):
    earlier = key_pos[None, :] <= query_pos[:, None]
    same_image = (key_seg[None, :] == query_seg[:, None]) & (query_seg[:, None] % 2 == 1)
    return earlier | same_image


def widen(source_rows, groups):
    tokens_dev = source_rows.shape[1]
    heads_here = source_rows.shape[2] // HEAD_DIM
    factor = max(1, groups // heads_here)
    spread = jnp.repeat(source_rows.reshape(1, tokens_dev, heads_here, HEAD_DIM), factor, axis=2)
    return spread.reshape(1, tokens_dev, heads_here * factor * HEAD_DIM)


def same_rows(row_ids):
    return row_ids


def update(current, allowed, query_block, key_block, value_block):
    maxima, denominators, weighted = current
    scores = jnp.einsum(
        "qkgd,skd->kgqs", query_block, key_block, preferred_element_type=jnp.float32
    )
    scores = jnp.where(allowed[None, None], scores * HEAD_DIM ** (-0.5), masked_score)
    new_max = jnp.maximum(maxima, jnp.max(scores, axis=3))
    weights = jnp.where(allowed[None, None], jnp.exp(scores - new_max[..., None]), 0.0)
    factor = jnp.exp(maxima - new_max)
    denominators = factor * denominators + jnp.sum(weights, axis=3)
    product = jnp.einsum(
        "kgqs,skd->kgqd",
        weights.astype(jnp.bfloat16),
        value_block,
        preferred_element_type=jnp.float32,
    )
    weighted = factor[..., None] * weighted + product
    return (new_max, denominators, weighted)


def keep_state(current, allowed, query_block, key_block, value_block):
    return current


def build_fold(query_rows, query_pos, tile_segment, key_position, kv_width):
    rows_total = query_rows.shape[0]
    kv_local = kv_width // HEAD_DIM
    group_size = query_rows.shape[1] // HEAD_DIM // kv_local
    shaped = query_rows.reshape(rows_total, kv_local, group_size, HEAD_DIM)
    query_seg = segment_of(query_pos, tile_segment)
    half_rows = rows_total // 2

    def fold_step(running, portion, offset):
        key_part, value_part = portion
        portion_rows = key_part.shape[0]
        block_rows = math.gcd(portion_rows, 512)
        block_total = portion_rows // block_rows
        key_blocks = key_part.reshape(block_total, block_rows, kv_local, HEAD_DIM)
        value_blocks = value_part.reshape(block_total, block_rows, kv_local, HEAD_DIM)

        def one_block(halves, inputs):
            key_block, value_block, block_number = inputs
            key_pos = key_position(
                block_number * block_rows + jnp.arange(block_rows, dtype=jnp.int32)
            )
            key_seg = segment_of(key_pos, tile_segment)
            results = []
            for half_index in range(2):
                row_low = half_index * half_rows
                row_high = row_low + half_rows
                allowed = visible(
                    query_pos[row_low:row_high], query_seg[row_low:row_high], key_pos, key_seg
                )
                results.append(
                    lax.cond(
                        jnp.any(allowed),
                        update,
                        keep_state,
                        halves[half_index],
                        allowed,
                        shaped[row_low:row_high],
                        key_block,
                        value_block,
                    )
                )
            return ((results[0], results[1]), None)

        running, unused = lax.scan(
            one_block, running, (key_blocks, value_blocks, jnp.arange(block_total, dtype=jnp.int32))
        )
        return running

    def empty_half():
        return (
            jnp.full((kv_local, group_size, half_rows), masked_score, jnp.float32),
            jnp.zeros((kv_local, group_size, half_rows), jnp.float32),
            jnp.zeros((kv_local, group_size, half_rows, HEAD_DIM), jnp.float32),
        )

    return (fold_step, (empty_half(), empty_half()))


def finish(running):
    outputs = [weighted / denominators[..., None] for maxima, denominators, weighted in running]
    joined = jnp.concatenate(outputs, axis=2)
    kv_local, group_size, rows_total, head_dim = joined.shape
    joined = jnp.transpose(joined, (2, 0, 1, 3)).reshape(
        rows_total, kv_local * group_size * head_dim
    )
    return joined.astype(jnp.bfloat16)


def local(queries, key_rows, value_rows, tile_segment):
    ulysses_count = lax.axis_size("ulysses")
    tokens_dev = queries.shape[1]
    block_len = tokens_dev * ulysses_count
    block_index = lax.axis_index("blk")
    local_rows = jnp.arange(block_len, dtype=jnp.int32)
    moved = (
        lax.all_to_all(queries, "ulysses", split_axis=2, concat_axis=1, tiled=True),
        lax.all_to_all(
            widen(key_rows, ulysses_count), "ulysses", split_axis=2, concat_axis=1, tiled=True
        ),
        lax.all_to_all(
            widen(value_rows, ulysses_count), "ulysses", split_axis=2, concat_axis=1, tiled=True
        ),
    )
    query_rows, key_local, value_local = (moved[0][0], moved[1][0], moved[2][0])
    query_pos = block_index * block_len + local_rows
    fold_step, initial = build_fold(
        query_rows, query_pos, tile_segment, same_rows, key_local.shape[1]
    )
    running = fold_step(
        initial,
        (
            lax.all_gather(key_local, "blk", axis=0, tiled=True),
            lax.all_gather(value_local, "blk", axis=0, tiled=True),
        ),
        jnp.int32(0),
    )
    attended = lax.all_to_all(
        finish(running)[None], "ulysses", split_axis=1, concat_axis=2, tiled=True
    )
    return attended


def solution(mesh):
    return jax.shard_map(
        local,
        mesh=mesh,
        in_specs=(
            P("blk", "ulysses", None),
            P("blk", "ulysses", None),
            P("blk", "ulysses", None),
            P(),
        ),
        out_specs=P("blk", "ulysses", None),
        check_vma=False,
    )
```

profile of v0, /device:TPU:4, one launch (start us, length us, event | category | flops | bytes accessed | tf_op | source)
XLA Modules:
  0.0 138.4 jit_solution(7677934682182908862)
XLA Ops:
  1.9 2.3 %reduce.4 = bf16[1024,64]{1,0:T(8,128)(2,1)S(1)} reduce(bf16[1024,1,64]{2,1,0:T(2,128)(2,1)S(1)} %bitcast.162, bf16[]{:T(256)} %broadcast.215), dimensions={1}, to_apply=%bitcast.126.reduce_sub_computation | reduce | bytes 262146
  5.1 5.8 %all-to-all-start = ((bf16[8,2,4096]{2,1,0:T(2,128)(2,1)}), bf16[8,2,4096]{2,1,0:T(2,128)(2,1)S(1)}, u32[]{:S(2)}, u32[]{:S(2)}) async-start(bf16[8,2,4096]{2,1,0:T(2,128)(2,1)} %reshape.154), calls=%async_computation | async-start | bytes 262144 | tf_op jit(solution)/shard_map/all_to_all | solution.py:136
  11.3 2.3 %reduce.5 = bf16[1024,64]{1,0:T(8,128)(2,1)S(1)} reduce(bf16[1024,1,64]{2,1,0:T(2,128)(2,1)S(1)} %bitcast.163, bf16[]{:T(256)} %broadcast.215), dimensions={1}, to_apply=%bitcast.128.reduce_sub_computation | reduce | bytes 262146
  14.5 3.7 %all-to-all-done = bf16[8,2,4096]{2,1,0:T(2,128)(2,1)S(1)} async-done(((bf16[8,2,4096]{2,1,0:T(2,128)(2,1)}), bf16[8,2,4096]{2,1,0:T(2,128)(2,1)S(1)}, u32[]{:S(2)}, u32[]{:S(2)}) %all-to-all-start) | async-done | bytes 131104 | tf_op jit(solution)/shard_map/all_to_all | solution.py:136
  18.2 3.4 %all-to-all-start.1 = ((bf16[8,2,4096]{2,1,0:T(2,128)(2,1)}), bf16[8,2,4096]{2,1,0:T(2,128)(2,1)S(1)}, u32[]{:S(2)}, u32[]{:S(2)}) async-start(bf16[8,2,4096]{2,1,0:T(2,128)(2,1)} %reshape.156), calls=%async_computation.1 | async-start | bytes 262144 | tf_op jit(solution)/shard_map/all_to_all | solution.py:139
  21.6 2.8 %copy.65 = bf16[1,64,4096]{1,0,2:T(2,128)(2,1)S(1)} copy(bf16[1,64,4096]{2,1,0:T(8,128)(2,1)S(1)} %copy-done) | data formatting | bytes 1048576 | tf_op args[0]
  24.4 22.5 %reduce.6 = bf16[4096,64]{1,0:T(8,128)(2,1)S(1)} reduce(bf16[4096,1,64]{2,1,0:T(2,128)(2,1)S(1)} %bitcast.152, bf16[]{:T(256)} %broadcast.215), dimensions={1}, to_apply=%bitcast.130.reduce_sub_computation | reduce | bytes 1048578
  46.9 1.5 %reshape.158 = bf16[8,2,16384]{2,1,0:T(2,128)(2,1)} reshape(bf16[4096,64]{1,0:T(8,128)(2,1)S(1)} %reduce.6) | data formatting | bytes 1048576
  48.5 5.9 %all-to-all-start.2 = ((bf16[8,2,16384]{2,1,0:T(2,128)(2,1)}), bf16[8,2,16384]{2,1,0:T(2,128)(2,1)}, u32[]{:S(2)}, u32[]{:S(2)}) async-start(bf16[8,2,16384]{2,1,0:T(2,128)(2,1)} %reshape.158), calls=%async_computation.2 | async-start | bytes 1048576 | tf_op jit(solution)/shard_map/all_to_all | solution.py:135
  55.9 6.7 %all_gather.6 = bf16[2048,128]{1,0:T(8,128)(2,1)S(1)} all-gather(bf16[512,128]{1,0:T(8,128)(2,1)S(1)} %bitcast.169), channel_id=1, replica_groups=mesh['ulysses'=8,'blk'=4] {'blk'}, dimensions={0}, use_global_device_ids=true | all-gather | bytes 655360 | tf_op jit(solution)/shard_map/all_gather | solution.py:151
  62.6 7.3 %all_gather.7 = bf16[2048,128]{1,0:T(8,128)(2,1)S(1)} all-gather(bf16[512,128]{1,0:T(8,128)(2,1)S(1)} %bitcast.170), channel_id=1, replica_groups=mesh['ulysses'=8,'blk'=4] {'blk'}, dimensions={0}, use_global_device_ids=true | all-gather | bytes 655360 | tf_op jit(solution)/shard_map/all_gather | solution.py:152
  69.9 4.1 %reshape.159 = bf16[4096,1,64]{2,1,0:T(2,128)(2,1)S(1)} reshape(bf16[8,2,16384]{2,1,0:T(2,128)(2,1)} %all-to-all-done.2) | data formatting | bytes 1048576
  74.0 3.6 %copy.66 = bf16[1,64,4096]{2,1,0:T(8,128)(2,1)} copy(bf16[1,64,4096]{1,0,2:T(2,128)(2,1)S(1)} %bitcast.151) | data formatting | bytes 1048576 | tf_op jit(solution)/shard_map/all_to_all | solution.py:135
  79.4 31.0 %while.23 = (s32[]{:T(128)}, f32[1,4,256]{2,1,0:T(4,128)S(1)}, f32[1,4,256]{2,1,0:T(4,128)S(1)}, f32[1,4,256,128]{3,2,1,0:T(8,128)S(1)}, f32[1,4,256]{2,1,0:T(4,...) while((s32[]{:T(128)}, f32[1,4,256]{2,1,0:T(4,128)S(1)}, ...), condition=%wide.region_13.14_spmd, body=%wide.region_1.13_spmd.sunk | while | flops 552381440 | bytes 17462768 | solution.py:103
  82.5 1.9 %conditional.5 = ((f32[1,4,256]{2,1,0:T(4,128)S(1)}, f32[1,4,256]{2,1,0:T(4,128)S(1)}, f32[1,4,256,128]{3,2,1,0:T(8,128)S(1)})) conditional(s32[]{:T(128)} %convert_element_type.47, (f32[1,4,256]{2,1,0:T(4,128)S(1)}, f32[1,4,256]{2,1,0:T(4,128)S(1)}, f32[1,4,256,128]{3,2,1,0:T(8,128)S(1)}) %tuple.82, (pred[256,512]{0,1:T(8,128)(4,1)S(1)}, ...), branch_computations={%region_9.9_spmd, %region_10.12_spmd} | conditional | flops 275516416 | bytes 8323104 | solution.py:90
  85.2 2.0 %conditional.4 = ((f32[1,4,256]{2,1,0:T(4,128)S(1)}, f32[1,4,256]{2,1,0:T(4,128)S(1)}, f32[1,4,256,128]{3,2,1,0:T(8,128)S(1)})) conditional(s32[]{:T(128)} %convert_element_type.46, (f32[1,4,256]{2,1,0:T(4,128)S(1)}, f32[1,4,256]{2,1,0:T(4,128)S(1)}, f32[1,4,256,128]{3,2,1,0:T(8,128)S(1)}) %tuple.80, (pred[256,512]{0,1:T(8,128)(4,1)S(1)}, ...), branch_computations={%region_4.4_spmd, %region_5.7_spmd} | conditional | flops 275516416 | bytes 8323104 | solution.py:90
  90.3 2.0 %conditional.5 = ((f32[1,4,256]{2,1,0:T(4,128)S(1)}, f32[1,4,256]{2,1,0:T(4,128)S(1)}, f32[1,4,256,128]{3,2,1,0:T(8,128)S(1)})) conditional(s32[]{:T(128)} %convert_element_type.47, (f32[1,4,256]{2,1,0:T(4,128)S(1)}, f32[1,4,256]{2,1,0:T(4,128)S(1)}, f32[1,4,256,128]{3,2,1,0:T(8,128)S(1)}) %tuple.82, (pred[256,512]{0,1:T(8,128)(4,1)S(1)}, ...), branch_computations={%region_9.9_spmd, %region_10.12_spmd} | conditional | flops 275516416 | bytes 8323104 | solution.py:90
  92.9 2.0 %conditional.4 = ((f32[1,4,256]{2,1,0:T(4,128)S(1)}, f32[1,4,256]{2,1,0:T(4,128)S(1)}, f32[1,4,256,128]{3,2,1,0:T(8,128)S(1)})) conditional(s32[]{:T(128)} %convert_element_type.46, (f32[1,4,256]{2,1,0:T(4,128)S(1)}, f32[1,4,256]{2,1,0:T(4,128)S(1)}, f32[1,4,256,128]{3,2,1,0:T(8,128)S(1)}) %tuple.80, (pred[256,512]{0,1:T(8,128)(4,1)S(1)}, ...), branch_computations={%region_4.4_spmd, %region_5.7_spmd} | conditional | flops 275516416 | bytes 8323104 | solution.py:90
  98.0 1.9 %conditional.5 = ((f32[1,4,256]{2,1,0:T(4,128)S(1)}, f32[1,4,256]{2,1,0:T(4,128)S(1)}, f32[1,4,256,128]{3,2,1,0:T(8,128)S(1)})) conditional(s32[]{:T(128)} %convert_element_type.47, (f32[1,4,256]{2,1,0:T(4,128)S(1)}, f32[1,4,256]{2,1,0:T(4,128)S(1)}, f32[1,4,256,128]{3,2,1,0:T(8,128)S(1)}) %tuple.82, (pred[256,512]{0,1:T(8,128)(4,1)S(1)}, ...), branch_computations={%region_9.9_spmd, %region_10.12_spmd} | conditional | flops 275516416 | bytes 8323104 | solution.py:90
  100.7 2.0 %conditional.4 = ((f32[1,4,256]{2,1,0:T(4,128)S(1)}, f32[1,4,256]{2,1,0:T(4,128)S(1)}, f32[1,4,256,128]{3,2,1,0:T(8,128)S(1)})) conditional(s32[]{:T(128)} %convert_element_type.46, (f32[1,4,256]{2,1,0:T(4,128)S(1)}, f32[1,4,256]{2,1,0:T(4,128)S(1)}, f32[1,4,256,128]{3,2,1,0:T(8,128)S(1)}) %tuple.80, (pred[256,512]{0,1:T(8,128)(4,1)S(1)}, ...), branch_computations={%region_4.4_spmd, %region_5.7_spmd} | conditional | flops 275516416 | bytes 8323104 | solution.py:90
  105.8 2.0 %conditional.5 = ((f32[1,4,256]{2,1,0:T(4,128)S(1)}, f32[1,4,256]{2,1,0:T(4,128)S(1)}, f32[1,4,256,128]{3,2,1,0:T(8,128)S(1)})) conditional(s32[]{:T(128)} %convert_element_type.47, (f32[1,4,256]{2,1,0:T(4,128)S(1)}, f32[1,4,256]{2,1,0:T(4,128)S(1)}, f32[1,4,256,128]{3,2,1,0:T(8,128)S(1)}) %tuple.82, (pred[256,512]{0,1:T(8,128)(4,1)S(1)}, ...), branch_computations={%region_9.9_spmd, %region_10.12_spmd} | conditional | flops 275516416 | bytes 8323104 | solution.py:90
  108.4 2.0 %conditional.4 = ((f32[1,4,256]{2,1,0:T(4,128)S(1)}, f32[1,4,256]{2,1,0:T(4,128)S(1)}, f32[1,4,256,128]{3,2,1,0:T(8,128)S(1)})) conditional(s32[]{:T(128)} %convert_element_type.46, (f32[1,4,256]{2,1,0:T(4,128)S(1)}, f32[1,4,256]{2,1,0:T(4,128)S(1)}, f32[1,4,256,128]{3,2,1,0:T(8,128)S(1)}) %tuple.80, (pred[256,512]{0,1:T(8,128)(4,1)S(1)}, ...), branch_computations={%region_4.4_spmd, %region_5.7_spmd} | conditional | flops 275516416 | bytes 8323104 | solution.py:90
  111.9 3.9 %reduce.7 = bf16[512,512]{1,0:T(8,128)(2,1)S(1)} reduce(bf16[512,1,512]{2,1,0:T(2,128)(2,1)S(1)} %bitcast.154, bf16[]{:T(256)} %broadcast.215), dimensions={1}, to_apply=%bitcast.132.reduce_sub_computation | reduce | bytes 1048578
  116.1 20.8 %all_to_all.63 = bf16[8,2,16384]{2,1,0:T(2,128)(2,1)S(1)} all-to-all(bf16[8,2,16384]{2,1,0:T(2,128)(2,1)S(1)} %reshape.160), channel_id=1, replica_groups=mesh['ulysses'=8,'blk'=4] {'ulysses'}, dimensions={0} | all-to-all | bytes 1048576 | tf_op jit(solution)/shard_map/all_to_all | solution.py:156
  (124 shorter events, 33.0 us)
Async XLA Ops:
  0.0 10.9 %copy-start.1 = (bf16[1,64,1024]{2,1,0:T(8,128)(2,1)S(1)}, bf16[1,64,1024]{2,1,0:T(8,128)(2,1)}, u32[]{:S(2)}) copy-start(bf16[1,64,1024]{2,1,0:T(8,128)(2,1)} %param.12) | copy-start | bytes 393220
  0.0 21.6 %copy-start = (bf16[1,64,4096]{2,1,0:T(8,128)(2,1)S(1)}, bf16[1,64,4096]{2,1,0:T(8,128)(2,1)}, u32[]{:S(2)}) copy-start(bf16[1,64,4096]{2,1,0:T(8,128)(2,1)} %param.10) | copy-start | bytes 1572868
  5.1 13.1 %all-to-all-start = ((bf16[8,2,4096]{2,1,0:T(2,128)(2,1)}), bf16[8,2,4096]{2,1,0:T(2,128)(2,1)S(1)}, u32[]{:S(2)}, u32[]{:S(2)}) async-start(bf16[8,2,4096]{2,1,0:T(2,128)(2,1)} %reshape.154), calls=%async_computation | async-start | bytes 262144 | tf_op jit(solution)/shard_map/all_to_all | solution.py:136
  18.2 30.3 %all-to-all-start.1 = ((bf16[8,2,4096]{2,1,0:T(2,128)(2,1)}), bf16[8,2,4096]{2,1,0:T(2,128)(2,1)S(1)}, u32[]{:S(2)}, u32[]{:S(2)}) async-start(bf16[8,2,4096]{2,1,0:T(2,128)(2,1)} %reshape.156), calls=%async_computation.1 | async-start | bytes 262144 | tf_op jit(solution)/shard_map/all_to_all | solution.py:139
  24.4 24.0 %copy-start.2 = (s32[16]{0:T(128)S(1)}, s32[16]{0:T(128)}, u32[]{:S(2)}) copy-start(s32[16]{0:T(128)} %param.13) | copy-start | bytes 196
  48.5 21.3 %all-to-all-start.2 = ((bf16[8,2,16384]{2,1,0:T(2,128)(2,1)}), bf16[8,2,16384]{2,1,0:T(2,128)(2,1)}, u32[]{:S(2)}, u32[]{:S(2)}) async-start(bf16[8,2,16384]{2,1,0:T(2,128)(2,1)} %reshape.158), calls=%async_computation.2 | async-start | bytes 1048576 | tf_op jit(solution)/shard_map/all_to_all | solution.py:135
where the time goes:
time: 139 us; the launch traced here: 138 us
  other arithmetic  40.5 us (29%)
  blocking collectives  34.7 us (25%)
  local copies, waits for them, and re-layouts  24.7 us (18%)
  starting transfers between devices  15.1 us (11%)
  matrix products  10.8 us (8%)
  loops' own time  8.49 us (6%)
  waiting for transfers between devices  3.74 us (3%)
    unnamed x4, other arithmetic  31 us
    all_to_all x1, blocking collectives, local(): lax.all_to_all(finish(running)[None], 'ulysses', split_axis=1, concat_axi...  20.8 us
    unnamed x22, local copies, waits for them, and re-layouts  15.4 us
    another operation x1, loops' own time, fold_step(): lax.scan(one_block, running, (key_blocks, value_blocks, jnp.arange(block_...  8.16 us
    all_gather x1, blocking collectives, local(): lax.all_gather(value_local, 'blk', axis=0, tiled=True)  7.26 us
    dot_general x8, matrix products, update(): jnp.einsum('kgqs,skd->kgqd', weights.astype(jnp.bfloat16), value_block, p...  6.93 us
    all_gather x1, blocking collectives, local(): lax.all_gather(key_local, 'blk', axis=0, tiled=True)  6.68 us
    all_to_all x1, starting transfers between devices, local(): lax.all_to_all(queries, 'ulysses', split_axis=2, concat_axis=1, tiled=True)  5.9 us
  transfers between devices with their start and end apart: 3, of which 1 were waited for; matrix products, arithmetic and copies ran while one was open for 23% of the time, Pallas kernels for 0%

commit v1 on v0

--- a/solution.py
+++ b/solution.py
@@ -7,6 +7,18 @@
 HEAD_DIM = 128
 TILE = 128
 masked_score = -1e30
+
+
+def in_blocks(array, dim, count):
+    lengths = array.shape
+    blocks = array.reshape(*lengths[:dim], count, lengths[dim] // count, *lengths[dim + 1 :])
+    return jnp.moveaxis(blocks, dim, 0)
+
+
+def joined_along(pieces, dim):
+    pieces = jnp.moveaxis(pieces, 0, dim)
+    lengths = pieces.shape
+    return pieces.reshape(*lengths[:dim], lengths[dim] * lengths[dim + 1], *lengths[dim + 2 :])
 
 
 def segment_of(positions, tile_segment):
@@ -153,9 +165,15 @@
         ),
         jnp.int32(0),
     )
-    attended = lax.all_to_all(
-        finish(running)[None], "ulysses", split_axis=1, concat_axis=2, tiled=True
-    )
+    x = finish(running)[None]
+    size, index = (lax.axis_size("ulysses"), lax.axis_index("ulysses"))
+    blocks = in_blocks(x, 1, size)
+    outs = [blocks[index]]
+    for step in range(1, size):
+        sent = blocks[index ^ step]
+        outs.append(lax.ppermute(sent, "ulysses", [(i, i ^ step) for i in range(size)]))
+    blocks = jnp.stack(outs)[index ^ jnp.arange(size)]
+    attended = joined_along(blocks, 2)
     return attended
 
 

time: 139 us -> 133 us (0.957); the launches traced: 138 us -> 131 us
  blocking collectives: 34.7 us -> 13.9 us
  starting transfers between devices: 15.1 us -> 26.5 us
  waiting for transfers between devices: 3.74 us -> 10.7 us
  other arithmetic: 40.5 us -> 36.7 us
    all_to_all x1 -> x0, blocking collectives: 20.8 us -> none  [local(): lax.all_to_all(finish(running)[None], 'ulysses', split_axis=1, concat_axi...]
    ppermute x0 -> x7, starting transfers between devices: none -> 11.3 us  [local(): lax.ppermute(sent, 'ulysses', [(i, i ^ step) for i in range(size)])]
    ppermute x0 -> x7, waiting for transfers between devices: none -> 6.91 us  [local(): lax.ppermute(sent, 'ulysses', [(i, i ^ step) for i in range(size)])]
    unnamed x4 -> x3, other arithmetic: 31 us -> 26.9 us
    unnamed x22 -> x25, local copies, waits for them, and re-layouts: 15.4 us -> 14.4 us
  transfers between devices with their start and end apart: 3 -> 10, of which waited for: 1 -> 3; matrix products, arithmetic and copies ran while one was open for 23% -> 24% of each run, Pallas kernels for 0% -> 0%
where the time goes in v1:
time: 133 us; the launch traced here: 131 us
  other arithmetic  36.7 us (28%)
  starting transfers between devices  26.5 us (20%)
  local copies, waits for them, and re-layouts  23.7 us (18%)
  blocking collectives  13.9 us (10%)
  matrix products  10.8 us (8%)
  waiting for transfers between devices  10.7 us (8%)
  loops' own time  8.25 us (6%)
    unnamed x3, other arithmetic  26.9 us
    unnamed x25, local copies, waits for them, and re-layouts  14.4 us
    ppermute x7, starting transfers between devices, local(): lax.ppermute(sent, 'ulysses', [(i, i ^ step) for i in range(size)])  11.3 us
    another operation x1, loops' own time, fold_step(): lax.scan(one_block, running, (key_blocks, value_blocks, jnp.arange(block_...  7.92 us
    all_gather x1, blocking collectives, local(): lax.all_gather(value_local, 'blk', axis=0, tiled=True)  7.26 us
    dot_general x8, matrix products, update(): jnp.einsum('kgqs,skd->kgqd', weights.astype(jnp.bfloat16), value_block, p...  6.93 us
    ppermute x7, waiting for transfers between devices, local(): lax.ppermute(sent, 'ulysses', [(i, i ^ step) for i in range(size)])  6.91 us
    all_gather x1, blocking collectives, local(): lax.all_gather(key_local, 'blk', axis=0, tiled=True)  6.68 us
  transfers between devices with their start and end apart: 10, of which 3 were waited for; matrix products, arithmetic and copies ran while one was open for 24% of the time, Pallas kernels for 0%

profile of v1, /device:TPU:4, one launch (start us, length us, event | category | flops | bytes accessed | tf_op | source)
XLA Modules:
  0.0 130.9 jit_solution(507074064834397227)
XLA Ops:
  1.8 2.3 %reduce.4 = bf16[1024,64]{1,0:T(8,128)(2,1)S(1)} reduce(bf16[1024,1,64]{2,1,0:T(2,128)(2,1)S(1)} %bitcast.188, bf16[]{:T(256)} %broadcast.254), dimensions={1}, to_apply=%bitcast.158.reduce_sub_computation | reduce | bytes 262146
  5.0 5.8 %all-to-all-start = ((bf16[8,2,4096]{2,1,0:T(2,128)(2,1)}), bf16[8,2,4096]{2,1,0:T(2,128)(2,1)S(1)}, u32[]{:S(2)}, u32[]{:S(2)}) async-start(bf16[8,2,4096]{2,1,0:T(2,128)(2,1)} %reshape.184), calls=%async_computation | async-start | bytes 262144 | tf_op jit(solution)/shard_map/all_to_all | solution.py:148
  11.2 2.3 %reduce.5 = bf16[1024,64]{1,0:T(8,128)(2,1)S(1)} reduce(bf16[1024,1,64]{2,1,0:T(2,128)(2,1)S(1)} %bitcast.189, bf16[]{:T(256)} %broadcast.254), dimensions={1}, to_apply=%bitcast.160.reduce_sub_computation | reduce | bytes 262146
  14.4 3.8 %all-to-all-done = bf16[8,2,4096]{2,1,0:T(2,128)(2,1)S(1)} async-done(((bf16[8,2,4096]{2,1,0:T(2,128)(2,1)}), bf16[8,2,4096]{2,1,0:T(2,128)(2,1)S(1)}, u32[]{:S(2)}, u32[]{:S(2)}) %all-to-all-start) | async-done | bytes 131104 | tf_op jit(solution)/shard_map/all_to_all | solution.py:148
  18.1 3.4 %all-to-all-start.1 = ((bf16[8,2,4096]{2,1,0:T(2,128)(2,1)}), bf16[8,2,4096]{2,1,0:T(2,128)(2,1)S(1)}, u32[]{:S(2)}, u32[]{:S(2)}) async-start(bf16[8,2,4096]{2,1,0:T(2,128)(2,1)} %reshape.186), calls=%async_computation.1 | async-start | bytes 262144 | tf_op jit(solution)/shard_map/all_to_all | solution.py:151
  21.6 2.8 %copy.57 = bf16[1,64,4096]{1,0,2:T(2,128)(2,1)S(1)} copy(bf16[1,64,4096]{2,1,0:T(8,128)(2,1)S(1)} %copy-done) | data formatting | bytes 1048576 | tf_op args[0]
  24.4 22.4 %reduce.6 = bf16[4096,64]{1,0:T(8,128)(2,1)S(1)} reduce(bf16[4096,1,64]{2,1,0:T(2,128)(2,1)S(1)} %bitcast.182, bf16[]{:T(256)} %broadcast.254), dimensions={1}, to_apply=%bitcast.162.reduce_sub_computation | reduce | bytes 1048578
  48.3 5.9 %all-to-all-start.2 = ((bf16[8,2,16384]{2,1,0:T(2,128)(2,1)}), bf16[8,2,16384]{2,1,0:T(2,128)(2,1)}, u32[]{:S(2)}, u32[]{:S(2)}) async-start(bf16[8,2,16384]{2,1,0:T(2,128)(2,1)} %reshape.188), calls=%async_computation.2 | async-start | bytes 1048576 | tf_op jit(solution)/shard_map/all_to_all | solution.py:147
  55.7 6.7 %all_gather.6 = bf16[2048,128]{1,0:T(8,128)(2,1)S(1)} all-gather(bf16[512,128]{1,0:T(8,128)(2,1)S(1)} %bitcast.197), channel_id=1, replica_groups=mesh['ulysses'=8,'blk'=4] {'blk'}, dimensions={0}, use_global_device_ids=true | all-gather | bytes 655360 | tf_op jit(solution)/shard_map/all_gather | solution.py:163
  62.4 7.3 %all_gather.7 = bf16[2048,128]{1,0:T(8,128)(2,1)S(1)} all-gather(bf16[512,128]{1,0:T(8,128)(2,1)S(1)} %bitcast.198), channel_id=1, replica_groups=mesh['ulysses'=8,'blk'=4] {'blk'}, dimensions={0}, use_global_device_ids=true | all-gather | bytes 655360 | tf_op jit(solution)/shard_map/all_gather | solution.py:164
  69.7 4.1 %reshape.189 = bf16[4096,1,64]{2,1,0:T(2,128)(2,1)S(1)} reshape(bf16[8,2,16384]{2,1,0:T(2,128)(2,1)} %all-to-all-done.2) | data formatting | bytes 1048576
  73.8 3.6 %copy.58 = bf16[1,64,4096]{2,1,0:T(8,128)(2,1)} copy(bf16[1,64,4096]{1,0,2:T(2,128)(2,1)S(1)} %bitcast.181) | data formatting | bytes 1048576 | tf_op jit(solution)/shard_map/all_to_all | solution.py:147
  79.2 30.7 %while.23 = (s32[]{:T(128)}, f32[1,4,256]{2,1,0:T(4,128)S(1)}, f32[1,4,256]{2,1,0:T(4,128)S(1)}, f32[1,4,256,128]{3,2,1,0:T(8,128)S(1)}, f32[1,4,256]{2,1,0:T(4,...) while((s32[]{:T(128)}, f32[1,4,256]{2,1,0:T(4,128)S(1)}, ...), condition=%wide.region_13.14_spmd, body=%wide.region_1.13_spmd.sunk | while | flops 552381440 | bytes 17462768 | solution.py:115
  84.9 2.0 %conditional.4 = ((f32[1,4,256]{2,1,0:T(4,128)S(1)}, f32[1,4,256]{2,1,0:T(4,128)S(1)}, f32[1,4,256,128]{3,2,1,0:T(8,128)S(1)})) conditional(s32[]{:T(128)} %convert_element_type.46, (f32[1,4,256]{2,1,0:T(4,128)S(1)}, f32[1,4,256]{2,1,0:T(4,128)S(1)}, f32[1,4,256,128]{3,2,1,0:T(8,128)S(1)}) %tuple.87, (pred[256,512]{0,1:T(8,128)(4,1)S(1)}, ...), branch_computations={%region_4.4_spmd, %region_5.7_spmd} | conditional | flops 275516416 | bytes 8323104 | solution.py:102
  90.0 2.0 %conditional.5 = ((f32[1,4,256]{2,1,0:T(4,128)S(1)}, f32[1,4,256]{2,1,0:T(4,128)S(1)}, f32[1,4,256,128]{3,2,1,0:T(8,128)S(1)})) conditional(s32[]{:T(128)} %convert_element_type.47, (f32[1,4,256]{2,1,0:T(4,128)S(1)}, f32[1,4,256]{2,1,0:T(4,128)S(1)}, f32[1,4,256,128]{3,2,1,0:T(8,128)S(1)}) %tuple.89, (pred[256,512]{0,1:T(8,128)(4,1)S(1)}, ...), branch_computations={%region_9.9_spmd, %region_10.12_spmd} | conditional | flops 275516416 | bytes 8323104 | solution.py:102
  92.6 2.0 %conditional.4 = ((f32[1,4,256]{2,1,0:T(4,128)S(1)}, f32[1,4,256]{2,1,0:T(4,128)S(1)}, f32[1,4,256,128]{3,2,1,0:T(8,128)S(1)})) conditional(s32[]{:T(128)} %convert_element_type.46, (f32[1,4,256]{2,1,0:T(4,128)S(1)}, f32[1,4,256]{2,1,0:T(4,128)S(1)}, f32[1,4,256,128]{3,2,1,0:T(8,128)S(1)}) %tuple.87, (pred[256,512]{0,1:T(8,128)(4,1)S(1)}, ...), branch_computations={%region_4.4_spmd, %region_5.7_spmd} | conditional | flops 275516416 | bytes 8323104 | solution.py:102
  97.7 2.0 %conditional.5 = ((f32[1,4,256]{2,1,0:T(4,128)S(1)}, f32[1,4,256]{2,1,0:T(4,128)S(1)}, f32[1,4,256,128]{3,2,1,0:T(8,128)S(1)})) conditional(s32[]{:T(128)} %convert_element_type.47, (f32[1,4,256]{2,1,0:T(4,128)S(1)}, f32[1,4,256]{2,1,0:T(4,128)S(1)}, f32[1,4,256,128]{3,2,1,0:T(8,128)S(1)}) %tuple.89, (pred[256,512]{0,1:T(8,128)(4,1)S(1)}, ...), branch_computations={%region_9.9_spmd, %region_10.12_spmd} | conditional | flops 275516416 | bytes 8323104 | solution.py:102
  100.3 2.0 %conditional.4 = ((f32[1,4,256]{2,1,0:T(4,128)S(1)}, f32[1,4,256]{2,1,0:T(4,128)S(1)}, f32[1,4,256,128]{3,2,1,0:T(8,128)S(1)})) conditional(s32[]{:T(128)} %convert_element_type.46, (f32[1,4,256]{2,1,0:T(4,128)S(1)}, f32[1,4,256]{2,1,0:T(4,128)S(1)}, f32[1,4,256,128]{3,2,1,0:T(8,128)S(1)}) %tuple.87, (pred[256,512]{0,1:T(8,128)(4,1)S(1)}, ...), branch_computations={%region_4.4_spmd, %region_5.7_spmd} | conditional | flops 275516416 | bytes 8323104 | solution.py:102
  105.4 2.0 %conditional.5 = ((f32[1,4,256]{2,1,0:T(4,128)S(1)}, f32[1,4,256]{2,1,0:T(4,128)S(1)}, f32[1,4,256,128]{3,2,1,0:T(8,128)S(1)})) conditional(s32[]{:T(128)} %convert_element_type.47, (f32[1,4,256]{2,1,0:T(4,128)S(1)}, f32[1,4,256]{2,1,0:T(4,128)S(1)}, f32[1,4,256,128]{3,2,1,0:T(8,128)S(1)}) %tuple.89, (pred[256,512]{0,1:T(8,128)(4,1)S(1)}, ...), branch_computations={%region_9.9_spmd, %region_10.12_spmd} | conditional | flops 275516416 | bytes 8323104 | solution.py:102
  108.0 2.0 %conditional.4 = ((f32[1,4,256]{2,1,0:T(4,128)S(1)}, f32[1,4,256]{2,1,0:T(4,128)S(1)}, f32[1,4,256,128]{3,2,1,0:T(8,128)S(1)})) conditional(s32[]{:T(128)} %convert_element_type.46, (f32[1,4,256]{2,1,0:T(4,128)S(1)}, f32[1,4,256]{2,1,0:T(4,128)S(1)}, f32[1,4,256,128]{3,2,1,0:T(8,128)S(1)}) %tuple.87, (pred[256,512]{0,1:T(8,128)(4,1)S(1)}, ...), branch_computations={%region_4.4_spmd, %region_5.7_spmd} | conditional | flops 275516416 | bytes 8323104 | solution.py:102
  111.1 2.1 %collective-permute-start = (bf16[1,64,512]{2,1,0:T(8,128)(2,1)S(1)}, bf16[1,64,512]{2,1,0:T(8,128)(2,1)S(1)}, u32[]{:S(2)}, u32[]{:S(2)}) collective-permute-start(bf16[1,64,512]{2,1,0:T(8,128)(2,1)S(1)} %get-tuple-element.476), channel_id=1, source_target_pairs={{0,4},{4,0},{8,12},{12,8},{16,20},{20,16},{24,28},{28,24},{1,5},{5... | collective-permute-start | bytes 196616 | tf_op jit(solution)/shard_map/ppermute | solution.py:174
  114.7 2.8 %collective-permute-start.3 = (bf16[1,64,512]{2,1,0:T(8,128)(2,1)S(1)}, bf16[1,64,512]{2,1,0:T(8,128)(2,1)S(1)}, u32[]{:S(2)}, u32[]{:S(2)}) collective-permute-start(bf16[1,64,512]{2,1,0:T(8,128)(2,1)S(1)} %get-tuple-element.473), channel_id=1, source_target_pairs={{0,16},{4,20},{8,24},{12,28},{16,0},{20,4},{24,8},{28,12},{1,17},{... | collective-permute-start | bytes 196616 | tf_op jit(solution)/shard_map/ppermute | solution.py:174
  119.0 3.3 %collective-permute-start.5 = (bf16[1,64,512]{2,1,0:T(8,128)(2,1)S(1)}, bf16[1,64,512]{2,1,0:T(8,128)(2,1)S(1)}, u32[]{:S(2)}, u32[]{:S(2)}) collective-permute-start(bf16[1,64,512]{2,1,0:T(8,128)(2,1)S(1)} %get-tuple-element.471), channel_id=1, source_target_pairs={{0,24},{4,28},{8,16},{12,20},{16,8},{20,12},{24,0},{28,4},{1,25},{... | collective-permute-start | bytes 196616 | tf_op jit(solution)/shard_map/ppermute | solution.py:174
  122.5 5.5 %collective-permute-done.4 = bf16[1,64,512]{2,1,0:T(8,128)(2,1)S(1)} collective-permute-done((bf16[1,64,512]{2,1,0:T(8,128)(2,1)S(1)}, bf16[1,64,512]{2,1,0:T(8,128)(2,1)S(1)}, u32[]{:S(2)}, u32[]{:S(2)}) %collective-permute-start.4) | collective-permute-done | bytes 65568 | tf_op jit(solution)/shard_map/ppermute | solution.py:174
  (143 shorter events, 40.3 us)
Async XLA Ops:
  0.0 10.8 %copy-start.1 = (bf16[1,64,1024]{2,1,0:T(8,128)(2,1)S(1)}, bf16[1,64,1024]{2,1,0:T(8,128)(2,1)}, u32[]{:S(2)}) copy-start(bf16[1,64,1024]{2,1,0:T(8,128)(2,1)} %param.12) | copy-start | bytes 393220
  0.0 21.5 %copy-start.2 = (s32[16]{0:T(128)S(1)}, s32[16]{0:T(128)}, u32[]{:S(2)}) copy-start(s32[16]{0:T(128)} %param.13) | copy-start | bytes 196
  0.0 21.6 %copy-start = (bf16[1,64,4096]{2,1,0:T(8,128)(2,1)S(1)}, bf16[1,64,4096]{2,1,0:T(8,128)(2,1)}, u32[]{:S(2)}) copy-start(bf16[1,64,4096]{2,1,0:T(8,128)(2,1)} %param.10) | copy-start | bytes 1572868
  5.0 13.1 %all-to-all-start = ((bf16[8,2,4096]{2,1,0:T(2,128)(2,1)}), bf16[8,2,4096]{2,1,0:T(2,128)(2,1)S(1)}, u32[]{:S(2)}, u32[]{:S(2)}) async-start(bf16[8,2,4096]{2,1,0:T(2,128)(2,1)} %reshape.184), calls=%async_computation | async-start | bytes 262144 | tf_op jit(solution)/shard_map/all_to_all | solution.py:148
  18.1 30.2 %all-to-all-start.1 = ((bf16[8,2,4096]{2,1,0:T(2,128)(2,1)}), bf16[8,2,4096]{2,1,0:T(2,128)(2,1)S(1)}, u32[]{:S(2)}, u32[]{:S(2)}) async-start(bf16[8,2,4096]{2,1,0:T(2,128)(2,1)} %reshape.186), calls=%async_computation.1 | async-start | bytes 262144 | tf_op jit(solution)/shard_map/all_to_all | solution.py:151
  48.3 21.4 %all-to-all-start.2 = ((bf16[8,2,16384]{2,1,0:T(2,128)(2,1)}), bf16[8,2,16384]{2,1,0:T(2,128)(2,1)}, u32[]{:S(2)}, u32[]{:S(2)}) async-start(bf16[8,2,16384]{2,1,0:T(2,128)(2,1)} %reshape.188), calls=%async_computation.2 | async-start | bytes 1048576 | tf_op jit(solution)/shard_map/all_to_all | solution.py:147
  111.1 7.9 %collective-permute-start = (bf16[1,64,512]{2,1,0:T(8,128)(2,1)S(1)}, bf16[1,64,512]{2,1,0:T(8,128)(2,1)S(1)}, u32[]{:S(2)}, u32[]{:S(2)}) collective-permute-start(bf16[1,64,512]{2,1,0:T(8,128)(2,1)S(1)} %get-tuple-element.476), channel_id=1, source_target_pairs={{0,4},{4,0},{8,12},{12,8},{16,20},{20,16},{24,28},{28,24},{1,5},{5... | collective-permute-start | bytes 196616 | tf_op jit(solution)/shard_map/ppermute | solution.py:174
  113.2 9.1 %collective-permute-start.1 = (bf16[1,64,512]{2,1,0:T(8,128)(2,1)S(1)}, bf16[1,64,512]{2,1,0:T(8,128)(2,1)S(1)}, u32[]{:S(2)}, u32[]{:S(2)}) collective-permute-start(bf16[1,64,512]{2,1,0:T(8,128)(2,1)S(1)} %get-tuple-element.475), channel_id=1, source_target_pairs={{0,8},{4,12},{8,0},{12,4},{16,24},{20,28},{24,16},{28,20},{1,9},{5... | collective-permute-start | bytes 196616 | tf_op jit(solution)/shard_map/ppermute | solution.py:174
  114.6 7.8 %collective-permute-start.2 = (bf16[1,64,512]{2,1,0:T(8,128)(2,1)S(1)}, bf16[1,64,512]{2,1,0:T(8,128)(2,1)S(1)}, u32[]{:S(2)}, u32[]{:S(2)}) collective-permute-start(bf16[1,64,512]{2,1,0:T(8,128)(2,1)S(1)} %get-tuple-element.474), channel_id=1, source_target_pairs={{0,12},{4,8},{8,4},{12,0},{16,28},{20,24},{24,20},{28,16},{1,13},{... | collective-permute-start | bytes 196616 | tf_op jit(solution)/shard_map/ppermute | solution.py:174
  114.7 7.8 %collective-permute-start.3 = (bf16[1,64,512]{2,1,0:T(8,128)(2,1)S(1)}, bf16[1,64,512]{2,1,0:T(8,128)(2,1)S(1)}, u32[]{:S(2)}, u32[]{:S(2)}) collective-permute-start(bf16[1,64,512]{2,1,0:T(8,128)(2,1)S(1)} %get-tuple-element.473), channel_id=1, source_target_pairs={{0,16},{4,20},{8,24},{12,28},{16,0},{20,4},{24,8},{28,12},{1,17},{... | collective-permute-start | bytes 196616 | tf_op jit(solution)/shard_map/ppermute | solution.py:174
  117.6 10.4 %collective-permute-start.4 = (bf16[1,64,512]{2,1,0:T(8,128)(2,1)S(1)}, bf16[1,64,512]{2,1,0:T(8,128)(2,1)S(1)}, u32[]{:S(2)}, u32[]{:S(2)}) collective-permute-start(bf16[1,64,512]{2,1,0:T(8,128)(2,1)S(1)} %get-tuple-element.472), channel_id=1, source_target_pairs={{0,20},{4,16},{8,28},{12,24},{16,4},{20,0},{24,12},{28,8},{1,21},{... | collective-permute-start | bytes 196616 | tf_op jit(solution)/shard_map/ppermute | solution.py:174
  119.0 9.0 %collective-permute-start.5 = (bf16[1,64,512]{2,1,0:T(8,128)(2,1)S(1)}, bf16[1,64,512]{2,1,0:T(8,128)(2,1)S(1)}, u32[]{:S(2)}, u32[]{:S(2)}) collective-permute-start(bf16[1,64,512]{2,1,0:T(8,128)(2,1)S(1)} %get-tuple-element.471), channel_id=1, source_target_pairs={{0,24},{4,28},{8,16},{12,20},{16,8},{20,12},{24,0},{28,4},{1,25},{... | collective-permute-start | bytes 196616 | tf_op jit(solution)/shard_map/ppermute | solution.py:174
  122.3 7.1 %collective-permute-start.6 = (bf16[1,64,512]{2,1,0:T(8,128)(2,1)S(1)}, bf16[1,64,512]{2,1,0:T(8,128)(2,1)S(1)}, u32[]{:S(2)}, u32[]{:S(2)}) collective-permute-start(bf16[1,64,512]{2,1,0:T(8,128)(2,1)S(1)} %get-tuple-element.470), channel_id=1, source_target_pairs={{0,28},{4,24},{8,20},{12,16},{16,12},{20,8},{24,4},{28,0},{1,29},{... | collective-permute-start | bytes 196616 | tf_op jit(solution)/shard_map/ppermute | solution.py:174
